TPU v7x, 32 devices: a whole 2x2x4 slice. The times are simulated.
32 devices in a mesh: dp: 2 (over x), my: 4 (over z), mx: 4 (over y, core).
Axes of the slice: x: 2, y: 2, z: 4, core: 2. Of those that a mesh axis runs over, the one named last changes fastest.
Arguments:
- tokens: bfloat16 [2, 256, 5120], P('dp', None, 'my'), parts along dimension 0
- ln_scale: bfloat16 [5120], P('my')
- w_in: bfloat16 [5120, 35840], P('my', 'mx')
- mlp_bias: bfloat16 [20480], P('mx')
- q_scale: bfloat16 [128], replicated
- k_scale: bfloat16 [128], replicated
- w_out: bfloat16 [25600, 5120], P('mx', 'my')
- attn_out_bias: bfloat16 [5120], P('my')
- mlp_out_bias: bfloat16 [5120], P('my')
Outputs:
- output: bfloat16 [2, 256, 5120], P('dp', None, 'my'), parts along dimension 0
There are 2 independent parts. A program takes and returns all parts, laid end to end along the dimension named above; an argument that names none is the same for every part.
All inputs are finite; a program needn't handle non-finite values.
Results may differ from a plain program's by a relative error of at most 0.0126557.
Values are sent between devices in bfloat16 or wider.
A program may use at most 1 GiB of HBM per device.

v0:
```python
import jax
import jax.numpy as jnp
from jax import lax
from jax.sharding import PartitionSpec as P


def head_norm(features, gain_vec):
    feat_f32 = features.astype(jnp.float32)
    centered = feat_f32 - jnp.mean(feat_f32, axis=-1, keepdims=True)
    variance = jnp.mean(jnp.square(centered), axis=-1, keepdims=True)
    return (centered * lax.rsqrt(variance + 1e-6) * gain_vec.astype(jnp.float32)).astype(jnp.bfloat16)


def mix_branches(projected, mlp_bias, q_scale, k_scale):
    batch_rows = projected.shape[0]
    seq_len = projected.shape[1]
    head_dim = q_scale.shape[0]
    ff_blk = mlp_bias.shape[0]
    qkv_blk = (projected.shape[2] - ff_blk) // 3
    head_shape = (batch_rows, seq_len, qkv_blk // head_dim, head_dim)
    queries = head_norm(projected[..., :qkv_blk].reshape(head_shape), q_scale)
    keys_n = head_norm(projected[..., qkv_blk:2 * qkv_blk].reshape(head_shape), k_scale)
    values = projected[..., 2 * qkv_blk:3 * qkv_blk].reshape(head_shape)
    logits = jnp.einsum('bqhd,bkhd->bhqk', queries, keys_n, preferred_element_type=jnp.float32) * head_dim ** -0.5
    attn_prob = jax.nn.softmax(logits, axis=-1).astype(jnp.bfloat16)
    mixed = jnp.einsum('bhqk,bkhd->bqhd', attn_prob, values, preferred_element_type=jnp.float32).astype(jnp.bfloat16)
    mlp_act = jax.nn.gelu(projected[..., 3 * qkv_blk:].astype(jnp.float32) + mlp_bias.astype(jnp.float32), approximate=False).astype(jnp.bfloat16)
    return jnp.concatenate([mixed.reshape(batch_rows, seq_len, qkv_blk), mlp_act], axis=-1)


def solution(mesh):
    width_shards = mesh.shape['my']

    def local_layer(tokens, ln_scale, w_in, mlp_bias, q_scale, k_scale, w_out, attn_out_bias, mlp_out_bias):
        width_total = tokens.shape[2] * width_shards
        tok_f32 = tokens.astype(jnp.float32)
        moments = jnp.stack([jnp.sum(tok_f32, axis=-1), jnp.sum(jnp.square(tok_f32), axis=-1)])
        moments = lax.psum(moments, 'my')
        row_mean = moments[0] / width_total
        variance = moments[1] / width_total - jnp.square(row_mean)
        inv_std = lax.rsqrt(variance + 1e-6)
        normed = ((tok_f32 - row_mean[..., None]) * inv_std[..., None] * ln_scale.astype(jnp.float32)).astype(jnp.bfloat16)
        partial_in = jnp.einsum('bsd,dc->bsc', normed, w_in, preferred_element_type=jnp.float32).astype(jnp.bfloat16)
        projected = lax.psum(partial_in, 'my')
        joined = mix_branches(projected, mlp_bias, q_scale, k_scale)
        partial_out = jnp.einsum('bsc,cd->bsd', joined, w_out, preferred_element_type=jnp.float32).astype(jnp.bfloat16)
        summed = lax.psum(partial_out, 'mx')
        result = summed.astype(jnp.float32) + attn_out_bias.astype(jnp.float32) + mlp_out_bias.astype(jnp.float32) + tok_f32
        return result.astype(jnp.bfloat16)

    specs_in = (P('dp', None, 'my'), P('my'), P('my', 'mx'), P('mx'), P(), P(), P('mx', 'my'), P('my'), P('my'))
    return jax.shard_map(local_layer, mesh=mesh, in_specs=specs_in, out_specs=P('dp', None, 'my'), check_vma=False)
```

profile of v0, /device:TPU:1, one launch (start us, length us, event | category | flops | bytes accessed | tf_op | source)
XLA Modules:
  0.0 273.8 jit_solution(3107274927061555276)
XLA Ops:
  6.5 0.0 all-reduce.3.cloned.1.call-start
  6.5 0.7 convert_element_type.136
  7.2 1.4 convert_reduce_fusion
  8.6 10.8 %psum.21 = f32[2,1,256]{2,1,0:T(1,128)S(1)} all-reduce(f32[2,1,256]{2,1,0:T(1,128)S(1)} %pad_maximum_fusion), channel_id=1, replica_groups=mesh['dp'=2,'my'=4,'mx'=4] {'my'}, use_global_device_ids=true, to_apply=%region_2.0 | all-reduce | flops 512 | bytes 4096 | tf_op jit(solution)/shard_map/psum | solution.py:38
  19.4 0.0 copy-start.1
  19.4 0.0 copy-start.4
  19.4 0.0 copy-start.5
  19.4 15.7 %fusion.1 = bf16[1,256,8960]{2,1,0:T(8,128)(2,1)} fusion(bf16[1280,8960]{1,0:T(8,128)(2,1)} %param.11, bf16[1,256,1280]{2,1,0:T(8,128)(2,1)} %param.9, f32[1280]{0:T(1024)S(1)} %convert_element_type.136, f32[256]{0:T(256)S(1)} %add_rsqrt_fusion.2, f32[256]{0:T(256)S(1)} %bitcast.42), kind=kOutput, calls=%fused_computation.2 | convolution fusion | flops 5875957760 | bytes 28187648 | tf_op jit(solution)/shard_map/bsd,dc->bsc/dot_general | solution.py:43
  35.1 0.0 all-reduce.3.cloned.1.call-update
  35.1 0.0 all-reduce.5.cloned.1.call-start
  35.2 0.0 copy-done.1
  35.2 0.0 copy-done.4
  35.2 0.0 copy-done.5
  35.2 166.5 %all-reduce.3.cloned.1.call-done = bf16[1,256,8960]{2,1,0:T(8,128)(2,1)} async-done(((bf16[1,256,8960]{2,1,0:T(8,128)(2,1)}), bf16[1,256,8960]{2,1,0:T(8,128)(2,1)}) %all-reduce.3.cloned.1.call-update) | async-done | bytes 4587536 | tf_op jit(solution)/shard_map/psum | solution.py:44
  201.8 2.8 %slice_convert_fusion = (f32[1,256,1280]{2,1,0:T(8,128)}, f32[1,256,1280]{2,1,0:T(8,128)S(1)}, bf16[1,256,1280]{2,1,0:T(8,128)(2,1)S(1)}) fusion(bf16[1,256,8960]{2,1,0:T(8,128)(2,1)} %all-reduce.3.cloned.1.call-done), kind=kLoop, calls=%fused_computation.52 | loop fusion | flops 655360 | bytes 5242880 | tf_op jit(solution)/shard_map/convert_element_type | solution.py:8
  204.6 0.2 copy.17
  204.8 0.4 copy.18
  205.2 1.7 copy.20
  207.0 0.1 reduce_sum.67
  207.1 0.2 multiply_reduce_fusion.1
  207.2 0.1 reduce_sum.65
  207.3 0.2 multiply_reduce_fusion.2
  207.5 0.7 fusion.29
  208.2 2.0 fusion.43
  210.2 0.4 convolution_convert_fusion.1
  210.6 0.2 copy.25
  210.9 12.8 %fusion.4 = bf16[1,256,5120]{2,1,0:T(8,128)(2,1)S(1)} fusion(bf16[1,256,8960]{2,1,0:T(8,128)(2,1)} %all-reduce.3.cloned.1.call-done, f32[5120]{0:T(1024)S(1)} %convert_element_type.157), kind=kLoop, calls=%fused_computation.6 | loop fusion | flops 87818240 | bytes 5263360 | tf_op jit(solution)/shard_map/convert_element_type | solution.py:27
  223.7 0.0 copy-start.2
  223.7 0.0 copy-start.3
  223.7 0.0 copy-start
  223.7 9.1 %fusion.19 = bf16[1,256,1280]{2,1,0:T(8,128)(2,1)} fusion(bf16[6400,1280]{1,0:T(8,128)(2,1)} %param.15, bf16[1,256,5120]{2,1,0:T(8,128)(2,1)S(1)} %fusion.4, bf16[1,256,1280]{2,1,0:T(8,128)(2,1)S(1)} %copy.25), kind=kOutput, calls=%fused_computation.32 | convolution fusion | flops 4201185280 | bytes 20316160 | tf_op jit(solution)/shard_map/bsc,cd->bsd/dot_general | solution.py:46
  232.9 0.0 all-reduce.5.cloned.1.call-update
  232.9 0.0 copy-done.2
  232.9 0.0 copy-done.3
  232.9 31.9 %all-reduce.5.cloned.1.call-done = bf16[1,256,1280]{2,1,0:T(8,128)(2,1)} async-done(((bf16[1,256,1280]{2,1,0:T(8,128)(2,1)}), bf16[1,256,1280]{2,1,0:T(8,128)(2,1)}) %all-reduce.5.cloned.1.call-update) | async-done | bytes 655376 | tf_op jit(solution)/shard_map/psum | solution.py:47
  264.8 0.0 copy-done
  264.8 2.2 fusion.27
  (11 shorter events, 0.1 us)
Async XLA Ops:
  6.5 195.3 %all-reduce.3.cloned.1.call-start = ((), (), s32[]{:S(2)}) async-start(), calls=%async_computation | async-start | bytes 9175040 | tf_op jit(solution)/shard_map/psum | solution.py:44
  19.4 15.8 %copy-start.1 = (bf16[5120]{0:T(1024)(128)(2,1)S(1)}, bf16[5120]{0:T(1024)(128)(2,1)}, u32[]{:S(2)}) copy-start(bf16[5120]{0:T(1024)(128)(2,1)} %param.12) | copy-start | bytes 30724
  19.4 15.8 %copy-start.4 = (bf16[128]{0:T(256)(128)(2,1)S(1)}, bf16[128]{0:T(256)(128)(2,1)}, u32[]{:S(2)}) copy-start(bf16[128]{0:T(256)(128)(2,1)} %param.14) | copy-start | bytes 772
  19.4 15.8 %copy-start.5 = (bf16[128]{0:T(256)(128)(2,1)S(1)}, bf16[128]{0:T(256)(128)(2,1)}, u32[]{:S(2)}) copy-start(bf16[128]{0:T(256)(128)(2,1)} %param.13) | copy-start | bytes 772
  35.1 229.7 %all-reduce.5.cloned.1.call-start = ((), (), s32[]{:S(2)}) async-start(), calls=%async_computation.1 | async-start | bytes 1310720 | tf_op jit(solution)/shard_map/psum | solution.py:47
  223.7 9.2 %copy-start.2 = (bf16[1280]{0:T(1024)(128)(2,1)S(1)}, bf16[1280]{0:T(1024)(128)(2,1)}, u32[]{:S(2)}) copy-start(bf16[1280]{0:T(1024)(128)(2,1)} %param.17) | copy-start | bytes 7684
  223.7 9.2 %copy-start.3 = (bf16[1280]{0:T(1024)(128)(2,1)S(1)}, bf16[1280]{0:T(1024)(128)(2,1)}, u32[]{:S(2)}) copy-start(bf16[1280]{0:T(1024)(128)(2,1)} %param.16) | copy-start | bytes 7684
  223.7 41.1 %copy-start = (bf16[1,256,1280]{2,1,0:T(8,128)(2,1)S(1)}, bf16[1,256,1280]{2,1,0:T(8,128)(2,1)}, u32[]{:S(2)}) copy-start(bf16[1,256,1280]{2,1,0:T(8,128)(2,1)} %param.9) | copy-start | bytes 1966084
Sparse Core Ops, SparseCore 0:
  35.3 166.4 all-reduce.2
  233.0 31.7 all-reduce.4
where the time goes:
time: 276 us; the launch traced here: 274 us
  waiting for transfers between devices  198 us (72%)
  matrix products  25.9 us (9%)
  other arithmetic  22.4 us (8%)
  between operations  13.6 us (5%)
  blocking collectives  10.8 us (4%)
    psum x1, waiting for transfers between devices, local_layer(): projected = lax.psum(partial_in, 'my')  167 us
    psum x1, waiting for transfers between devices, local_layer(): summed = lax.psum(partial_out, 'mx')  31.9 us
    dot_general x1, matrix products, local_layer(): jnp.einsum('bsd,dc->bsc', normed, w_in, preferred_element_type=jnp.float32)  15.7 us
    convert_element_type x1, other arithmetic, mix_branches(): jax.nn.gelu(projected[..., 3 * qkv_blk:].astype(jnp.float32) + mlp_bias.a...  12.8 us
    psum x1, blocking collectives, local_layer(): moments = lax.psum(moments, 'my')  10.8 us
    dot_general x1, matrix products, local_layer(): jnp.einsum('bsc,cd->bsd', joined, w_out, preferred_element_type=jnp.float32)  9.14 us
  transfers between devices with their start and end apart: 2, of which 2 were waited for; matrix products, arithmetic and copies ran while one was open for 0% of the time, Pallas kernels for 0%

commit v1 on v0

v1 whole, which is shorter than its diff:
```python
import jax
import jax.numpy as jnp
from jax import lax
from jax.experimental import pallas as pl
from jax.experimental.pallas import tpu as pltpu
from jax.sharding import PartitionSpec as P

MESH = pl.DeviceIdType.MESH
F32 = jnp.float32
BF16 = jnp.bfloat16

SEQ = 256
DL = 1280
DTOT = 5120
HD = 128
QKV_W = 1280
HALF_H = 5
FFB = 5120
CW = 512
NJ = FFB // CW
UR = 32
GROUPS = ((0, 128), (128, 96), (224, 32))

NQ = 3 * HALF_H * 2
NA = HALF_H * 2
NM = NJ * (SEQ // UR)
NU = NQ + NA + NM
HOP = 5
A0 = 48

FAR, NEAR, MLP = 0, NQ, 2 * NQ
EARLY = 2 * NQ + NM
LATE = EARLY + NU
NBUF = LATE + NU

P_LN, P_OB, P_QK = NJ, NJ + 3, NJ + 6


def head_norm(feat, gain):
    feat = feat.astype(F32)
    cent = feat - jnp.mean(feat, axis=-1, keepdims=True)
    var = jnp.mean(jnp.square(cent), axis=-1, keepdims=True)
    return (cent * lax.rsqrt(var + 1e-6) * gain).astype(BF16)


def layer_kernel(tok, win, wout, prm, out, buf, wi, wo, xv, zv, acc, att, qkv, act, mxb, stat,
                 wsem, xsem, ssem, rsem, tsend, trecv, msend, mrecv, osem):
    dp = lax.axis_index("dp")
    z = lax.axis_index("my")
    mx = lax.axis_index("mx")
    low = z < 2
    k = jnp.where(low, z, 3 - z)
    side = jnp.where(low, 0, 1)
    inner = jnp.where(low, z + 1, z - 1)
    outer = jnp.where(k == 0, inner, jnp.where(low, z - 1, z + 1))
    core_peer = mx + 1 - 2 * (mx % 2)
    y_peer = (mx + 2) % 4
    near = HALF_H * side
    far = HALF_H * (1 - side)

    def win_copy(col, width, idx):
        cols = pl.ds(pl.multiple_of(col, 128), width)
        return pltpu.make_async_copy(win.at[:, cols], wi.at[:, cols], wsem.at[idx])

    def qkv_copy(t, base, idx):
        return win_copy(t * QKV_W + base * HD, HALF_H * HD, idx)

    def up_copy(j):
        return win_copy(3 * QKV_W + j * CW, CW, 6 + j)

    def attn_w_copy():
        return pltpu.make_async_copy(wout.at[pl.ds(0, QKV_W)], wo.at[pl.ds(0, QKV_W)], wsem.at[6 + NJ])

    def down_copy(j):
        rows = pl.ds(pl.multiple_of(QKV_W + j * CW, 128), CW)
        return pltpu.make_async_copy(wout.at[rows], wo.at[rows], wsem.at[7 + NJ + j])

    x_copy = pltpu.make_async_copy(tok.at[0], xv, xsem)
    x_copy.start()
    for t in range(3):
        qkv_copy(t, far, t).start()
    for t in range(3):
        qkv_copy(t, near, 3 + t).start()
    for j in range(NJ):
        up_copy(j).start()
    attn_w_copy().start()
    for j in range(NJ):
        down_copy(j).start()

    barrier = pltpu.get_barrier_semaphore()
    for i in range(1, 4):
        pl.semaphore_signal(barrier, inc=1, device_id=(dp, (z + i) % 4, mx), device_id_type=MESH)
    for peer in (core_peer, y_peer):
        pl.semaphore_signal(barrier, inc=1, device_id=(dp, z, peer), device_id_type=MESH)

    acc[...] = jnp.zeros_like(acc)

    x_copy.wait()
    xf = xv[...].astype(F32)
    mu = jnp.sum(xf, axis=1, keepdims=True) * (1.0 / DL)
    m2 = jnp.sum(jnp.square(xf - mu), axis=1, keepdims=True)
    lane = lax.broadcasted_iota(jnp.int32, (SEQ, 128), 1)
    stat[z] = jnp.where(lane == 0, mu, m2).T[:8]
    pl.semaphore_wait(barrier, 5)

    def stat_copy(i):
        return pltpu.make_async_remote_copy(
            src_ref=stat.at[z], dst_ref=stat.at[z], send_sem=tsend.at[i], recv_sem=trecv.at[z],
            device_id=(dp, (z + i) % 4, mx), device_id_type=MESH)

    for i in (3, 2, 1):
        stat_copy(i).start()
    for t in range(3):
        qkv_copy(t, far, t).wait()
    for i in range(1, 4):
        src = (z + i) % 4
        pltpu.make_async_copy(stat.at[src], stat.at[src], trecv.at[src]).wait()
    means = [stat[i][0:1] for i in range(4)]
    devs = [stat[i][1:2] for i in range(4)]
    mean = (means[0] + means[1] + means[2] + means[3]) * 0.25
    m2_all = devs[0] + devs[1] + devs[2] + devs[3]
    for i in range(4):
        m2_all = m2_all + DL * jnp.square(means[i] - mean)
    inv = lax.rsqrt(m2_all * (1.0 / DTOT) + 1e-6)
    row = lax.broadcasted_iota(jnp.int32, (128, SEQ), 0)
    cols2 = jnp.where(row == 0, mean, inv).T
    ln_gain = jnp.concatenate([prm[P_LN:P_LN + 1, :], prm[P_LN + 1:P_LN + 2, :], prm[P_LN + 2:P_LN + 3, :256]], axis=1)
    zv[...] = ((xv[...].astype(F32) - cols2[:, 0:1]) * cols2[:, 1:2] * ln_gain).astype(BF16)

    def qkv_piece(p, base, first):
        col = (p % 3) * QKV_W + (base + p // 3) * HD
        part = jnp.dot(zv[...], wi[:, pl.ds(pl.multiple_of(col, 128), HD)], preferred_element_type=F32).astype(BF16)
        for half in range(2):
            for i in range(4):
                r0 = half * 128 + UR * i
                buf[first + 2 * p + half, :, HD * i:HD * (i + 1)] = part[r0:r0 + UR]

    def mlp_chunk(j):
        up_copy(j).wait()
        col = 3 * QKV_W + j * CW
        part = jnp.dot(zv[...], wi[:, pl.ds(pl.multiple_of(col, 128), CW)], preferred_element_type=F32).astype(BF16)
        base = 0
        for r0, rows in GROUPS:
            per = rows // UR
            for i in range(per):
                buf[MLP + base + per * j + i] = part[r0 + UR * i:r0 + UR * (i + 1)]
            base += NJ * per

    def unit_copy(src, dst, which, dst_which, u, target):
        return pltpu.make_async_remote_copy(
            src_ref=buf.at[src], dst_ref=buf.at[dst], send_sem=ssem.at[which, u], recv_sem=rsem.at[dst_which, u],
            device_id=(dp, target, mx), device_id_type=MESH)

    def arrival(slot, which, u):
        return pltpu.make_async_copy(buf.at[slot], buf.at[slot], rsem.at[which, u])

    def kind(u):
        is_q = u < NQ
        is_a = jnp.logical_and(u >= A0, u < A0 + NA)
        m = u - NQ - jnp.where(u >= A0 + NA, NA, 0)
        return is_q, is_a, m

    def put_attention(which, u, unit):
        head = (u - A0) // 2
        half = (u - A0) % 2
        for i in range(4):
            r0 = pl.multiple_of(half * 128 + UR * i, UR)
            att[which, pl.ds(r0, UR), pl.ds(pl.multiple_of(head * HD, HD), HD)] = unit[:, HD * i:HD * (i + 1)]

    def activate(m, h, j):
        pre = h.astype(BF16).astype(F32) + prm[pl.ds(j, 1), :]
        return (0.5 * pre * (1.0 + lax.erf(pre * (0.5 ** 0.5)))).astype(BF16)

    def down(g, j):
        r0, rows = GROUPS[g]
        w0 = pl.multiple_of(QKV_W + j * CW, 128)
        for n in range(DL // 256):
            acc[r0:r0 + rows, 256 * n:256 * (n + 1)] += jnp.dot(
                act[0:rows, :], wo[pl.ds(w0, CW), 256 * n:256 * (n + 1)], preferred_element_type=F32)

    def mx_copy(step, g):
        rows = pl.ds(GROUPS[g][0], GROUPS[g][1])
        return pltpu.make_async_remote_copy(
            src_ref=mxb.at[2 * step, rows], dst_ref=mxb.at[2 * step + 1, rows],
            send_sem=msend.at[step, g], recv_sem=mrecv.at[step, g],
            device_id=(dp, z, (core_peer, y_peer)[step]), device_id_type=MESH)

    def out_copy(g):
        rows = pl.ds(GROUPS[g][0], GROUPS[g][1])
        return pltpu.make_async_copy(xv.at[rows], out.at[0, rows], osem.at[g])

    def reduce_a(g):
        r0, rows = GROUPS[g]
        mxb[0, r0:r0 + rows] = acc[r0:r0 + rows].astype(BF16)
        mx_copy(0, g).start()

    def reduce_b(g):
        r0, rows = GROUPS[g]
        mx_copy(0, g).wait()
        mxb[2, r0:r0 + rows] = (mxb[0, r0:r0 + rows].astype(F32) + mxb[1, r0:r0 + rows].astype(F32)).astype(BF16)
        mx_copy(1, g).start()

    def reduce_c(g):
        r0, rows = GROUPS[g]
        mx_copy(1, g).wait()
        total = mxb[2, r0:r0 + rows].astype(F32) + mxb[3, r0:r0 + rows].astype(F32)
        bias = jnp.concatenate([prm[P_OB:P_OB + 1, :], prm[P_OB + 1:P_OB + 2, :], prm[P_OB + 2:P_OB + 3, :256]], axis=1)
        xv[r0:r0 + rows] = (total + bias + xv[r0:r0 + rows].astype(F32)).astype(BF16)
        out_copy(g).start()

    qkv_piece(0, far, FAR)

    late_lag = (3 - k) * HOP
    group_end = []
    done = 0
    for _, rows in GROUPS:
        done += NJ * rows // UR
        group_end.append(NQ + NA + done - 1)

    def step(s, carry):
        @pl.when(s < 14)
        def _():
            qkv_piece(s + 1, far, FAR)

        @pl.when(s == 2)
        def _():
            for t in range(3):
                qkv_copy(t, near, 3 + t).wait()

        @pl.when(jnp.logical_and(s >= 2, s < 17))
        def _():
            qkv_piece(s - 2, near, NEAR)

        @pl.when(jnp.logical_and(s >= 17, s < 17 + NJ))
        def _():
            mlp_chunk(s - 17)

        ue = s - k * HOP

        @pl.when(jnp.logical_and(ue >= 0, ue < NU))
        def _():
            is_q, is_a, m = kind(ue)
            own = jnp.where(is_q, FAR + ue, MLP + m)
            slot = EARLY + ue

            @pl.when(k == 1)
            def _():
                arrival(slot, 0, ue).wait()

                @pl.when(jnp.logical_not(is_a))
                def _():
                    buf[slot] = (buf[slot].astype(F32) + buf[own].astype(F32)).astype(BF16)

            src = jnp.where(jnp.logical_or(k == 1, is_a), slot, own)
            unit_copy(src, jnp.where(k == 0, EARLY, LATE) + ue, 0, k, ue, inner).start()

            @pl.when(jnp.logical_and(k == 1, is_a))
            def _():
                put_attention(0, ue, buf[slot])

        ul = s - late_lag

        @pl.when(jnp.logical_and(ul >= 0, ul < NU))
        def _():
            is_q, is_a, m = kind(ul)
            own = jnp.where(is_q, NEAR + ul, MLP + m)
            slot = LATE + ul
            arrival(slot, 1, ul).wait()
            is_m = jnp.logical_not(jnp.logical_or(is_q, is_a))
            g = jnp.where(m < 40, 0, jnp.where(m < 70, 1, 2))
            per = jnp.where(g == 0, 4, jnp.where(g == 1, 3, 1))
            mm = m - jnp.where(g == 0, 0, jnp.where(g == 1, 40, 70))
            j = jnp.where(g == 0, mm // 4, jnp.where(g == 1, mm // 3, mm))
            i = mm - per * j

            @pl.when(is_m)
            def _():
                other = jnp.where(k == 0, own, EARLY + ul)
                h = buf[slot].astype(F32) + buf[other].astype(F32)
                act[pl.ds(pl.multiple_of(i * UR, UR), UR), :] = activate(m, h, j)

            @pl.when(k == 1)
            def _():
                @pl.when(jnp.logical_not(is_a))
                def _():
                    buf[slot] = (buf[slot].astype(F32) + buf[own].astype(F32)).astype(BF16)

                unit_copy(slot, slot, 1, 1, ul, outer).start()

            @pl.when(is_a)
            def _():
                put_attention(1, ul, buf[slot])

            @pl.when(jnp.logical_and(k == 0, is_q))
            def _():
                whole = (buf[slot].astype(F32) + buf[own].astype(F32)).astype(BF16)
                p = ul // 2
                half = ul % 2
                for q in range(4):
                    r0 = pl.multiple_of(half * 128 + UR * q, UR)
                    qkv[p, pl.ds(r0, UR), :] = whole[:, HD * q:HD * (q + 1)]

            for gg in range(3):
                @pl.when(jnp.logical_and(is_m, jnp.logical_and(g == gg, i == per - 1)))
                def _():
                    if gg == 0:
                        down_copy(j).wait()
                    down(gg, j)

            for gg in range(3):
                @pl.when(ul == group_end[gg])
                def _():
                    reduce_a(gg)

            for gg in range(2):
                @pl.when(ul == group_end[gg] + 4)
                def _():
                    reduce_b(gg)

            @pl.when(ul == group_end[0] + 18)
            def _():
                reduce_c(0)

        head = (ul + 1) // 6 - 1

        @pl.when(jnp.logical_and(jnp.logical_and(k == 0, ul < NQ), jnp.logical_and(ul >= 5, (ul + 1) % 6 == 0)))
        def _():
            query = head_norm(qkv[3 * head], prm[P_QK:P_QK + 1, 0:HD])
            key = head_norm(qkv[3 * head + 1], prm[P_QK:P_QK + 1, HD:2 * HD])
            logits = lax.dot_general(query, key, (((1,), (1,)), ((), ())), preferred_element_type=F32) * (HD ** -0.5)
            expo = jnp.exp(logits - jnp.max(logits, axis=-1, keepdims=True))
            prob = (expo / jnp.sum(expo, axis=-1, keepdims=True)).astype(BF16)
            mixed = jnp.dot(prob, qkv[3 * head + 2], preferred_element_type=F32).astype(BF16)
            att[0, :, pl.ds(pl.multiple_of(head * HD, HD), HD)] = mixed
            for half in range(2):
                for q in range(4):
                    r0 = half * 128 + UR * q
                    buf[EARLY + A0 + 2 * head + half, :, HD * q:HD * (q + 1)] = mixed[r0:r0 + UR]

        n = ul - (A0 + NA)

        @pl.when(n == 0)
        def _():
            attn_w_copy().wait()

        @pl.when(jnp.logical_and(n >= 0, n < DL // 256))
        def _():
            cols = pl.ds(pl.multiple_of(n * 256, 256), 256)
            near_rows = pl.ds(pl.multiple_of(near * HD, HD), HALF_H * HD)
            far_rows = pl.ds(pl.multiple_of(far * HD, HD), HALF_H * HD)
            acc[:, cols] += (jnp.dot(att[0], wo[near_rows, cols], preferred_element_type=F32)
                             + jnp.dot(att[1], wo[far_rows, cols], preferred_element_type=F32))

        return carry

    lax.fori_loop(0, NU + late_lag, step, 0)
    reduce_c(1)
    reduce_b(2)

    def drain(u, carry):
        unit_copy(0, 0, 0, 0, u, inner).wait_send()

        @pl.when(k == 1)
        def _():
            unit_copy(0, 0, 1, 1, u, outer).wait_send()

        return carry

    lax.fori_loop(0, NU, drain, 0)
    for i in range(1, 4):
        stat_copy(i).wait_send()
    reduce_c(2)
    for g in range(3):
        out_copy(g).wait()


def solution(mesh):
    def local_layer(tokens, ln_scale, w_in, mlp_bias, q_scale, k_scale, w_out, attn_out_bias, mlp_out_bias):
        pad = jnp.zeros((256,), F32)
        table = jnp.concatenate([
            mlp_bias.astype(F32), ln_scale.astype(F32), pad,
            attn_out_bias.astype(F32) + mlp_out_bias.astype(F32), pad,
            q_scale.astype(F32), k_scale.astype(F32), pad]).reshape(-1, CW)
        dma = pltpu.SemaphoreType.DMA
        anyspace = pl.BlockSpec(memory_space=pl.ANY)
        return pl.pallas_call(
            layer_kernel,
            out_shape=jax.ShapeDtypeStruct((1, SEQ, DL), BF16),
            in_specs=[anyspace, anyspace, anyspace, pl.BlockSpec(memory_space=pltpu.VMEM)],
            out_specs=anyspace,
            scratch_shapes=[
                pltpu.VMEM((NBUF, UR, CW), BF16),
                pltpu.VMEM((DL, 3 * QKV_W + FFB), BF16),
                pltpu.VMEM((QKV_W + FFB, DL), BF16),
                pltpu.VMEM((SEQ, DL), BF16),
                pltpu.VMEM((SEQ, DL), BF16),
                pltpu.VMEM((SEQ, DL), F32),
                pltpu.VMEM((2, SEQ, HALF_H * HD), BF16),
                pltpu.VMEM((3 * HALF_H, SEQ, HD), BF16),
                pltpu.VMEM((128, CW), BF16),
                pltpu.VMEM((4, SEQ, DL), BF16),
                pltpu.VMEM((4, 8, SEQ), F32),
                dma((7 + 2 * NJ,)),
                dma,
                dma((2, NU)),
                dma((2, NU)),
                dma((4,)),
                dma((4,)),
                dma((2, 3)),
                dma((2, 3)),
                dma((3,)),
            ],
            compiler_params=pltpu.CompilerParams(
                collective_id=0, has_side_effects=True, vmem_limit_bytes=67043328),
            name="layer",
        )(tokens, w_in, w_out, table)

    specs_in = (P('dp', None, 'my'), P('my'), P('my', 'mx'), P('mx'), P(), P(), P('mx', 'my'), P('my'), P('my'))
    return jax.shard_map(local_layer, mesh=mesh, in_specs=specs_in, out_specs=P('dp', None, 'my'), check_vma=False)
```

time: 276 us -> 133 us (0.48)
  waiting for transfers between devices: 198 us -> 0 us
  Pallas kernels: 0 us -> 124 us
  matrix products: 25.9 us -> 0 us
  other arithmetic: 22.4 us -> 3.43 us
  between operations: 13.6 us -> 0.02 us
  blocking collectives: 10.8 us -> 0 us
    psum x2 -> x0, waiting for transfers between devices: 198 us -> none  [the longest x1 167 us: local_layer(): projected = lax.psum(partial_in, 'my')]
    pallas_call x0 -> x1, Pallas kernels: none -> 124 us  [local_layer(): pl.pallas_call(layer_kernel, out_shape=jax.ShapeDtypeStruct((1, SEQ, DL),...]
    dot_general x4 -> x0, matrix products: 25.9 us -> none  [the longest x1 15.7 us: local_layer(): jnp.einsum('bsd,dc->bsc', normed, w_in, preferred_element_type=jnp.float32)]
    convert_element_type x9 -> x0, other arithmetic: 18.5 us -> none  [the longest x1 12.8 us: mix_branches(): jax.nn.gelu(projected[..., 3 * qkv_blk:].astype(jnp.float32) + mlp_bias.a...]
    psum x1 -> x0, blocking collectives: 10.8 us -> none  [local_layer(): moments = lax.psum(moments, 'my')]
    unnamed x0 -> x5, other arithmetic: none -> 3.43 us
  transfers between devices with their start and end apart: 2 -> 0, of which waited for: 2 -> 0; matrix products, arithmetic and copies ran while one was open for 0% -> 0% of each run, Pallas kernels for 0% -> 0%
where the time goes in v1:
time: 133 us; the launch traced here: 131 us
  Pallas kernels  124 us (93%)
  other arithmetic  3.43 us (3%)
  local copies, waits for them, and re-layouts  2.61 us (2%)
    pallas_call x1, Pallas kernels, local_layer(): pl.pallas_call(layer_kernel, out_shape=jax.ShapeDtypeStruct((1, SEQ, DL),...  124 us
    unnamed x5, other arithmetic  3.43 us

profile of v1, /device:TPU:1, one launch (start us, length us, event | category | flops | bytes accessed | tf_op | source)
XLA Modules:
  0.0 130.5 jit_solution(12777673460135698080)
XLA Ops:
  0.0 0.7 convert_dynamic-update-slice_fusion
  0.7 0.7 convert_dynamic-update-slice_fusion.1
  1.4 0.7 add_dynamic-update-slice_fusion
  2.1 0.7 constant_dynamic-update-slice_fusion.2
  2.8 0.7 constant_dynamic-update-slice_fusion.1
  3.5 0.6 reshape.3.prm
  4.1 124.4 %layer.1 = bf16[1,256,1280]{2,1,0:T(8,128)(2,1)} custom-call(bf16[1,256,1280]{2,1,0:T(8,128)(2,1)} %tok.1, bf16[1280,8960]{1,0:T(8,128)(2,1)} %win.1, bf16[6400,1280]{1,0:T(8,128)(2,1)} %wout.1, f32[17,512]{1,0:T(8,128)} %reshape.3.prm), custom_call_target="tpu_custom_call" | custom-call | tf_op jit(solution)/shard_map/layer/pallas_call | solution.py:386
  128.5 2.0 %copy.18 = bf16[1,256,1280]{2,1,0:T(8,128)(2,1)} copy(bf16[1,256,1280]{2,1,0:T(8,128)(2,1)} %layer.1) | data formatting | bytes 1310720
  (3 shorter events, 0.0 us)

commit v2 on v1

v2 whole, which is shorter than its diff:
```python
import jax
import jax.numpy as jnp
from jax import lax
from jax.experimental import pallas as pl
from jax.experimental.pallas import tpu as pltpu
from jax.sharding import PartitionSpec as P

MESH = pl.DeviceIdType.MESH
F32 = jnp.float32
BF16 = jnp.bfloat16

SEQ = 256
DL = 1280
DTOT = 5120
HD = 128
QKV_W = 1280
HALF_H = 5
SIDE_W = HALF_H * HD
FFB = 5120
CW = 512
NJ = FFB // CW
UR = 64
GROUPS = ((0, 128, 0), (128, 64, 20), (192, 32, 30), (224, 32, 35))
NG = len(GROUPS)

NQ = 3 * HALF_H
NA = HALF_H
NM = 40
NU = NQ + NA + NM
HOP = 3
A0 = 24
GROUP_END = (39, 49, 54, 59)

FAR, NEAR, MLP = 0, NQ, 2 * NQ
EARLY = 2 * NQ + NM
LATE = EARLY + NU
NBUF = LATE + NU
BLOCKS = tuple((t, c, w) for t in range(3) for c, w in ((0, 256), (256, 256), (512, 128)))


def head_norm(feat, gain):
    feat = feat.astype(F32)
    cent = feat - jnp.mean(feat, axis=-1, keepdims=True)
    var = jnp.mean(jnp.square(cent), axis=-1, keepdims=True)
    return (cent * lax.rsqrt(var + 1e-6) * gain).astype(BF16)


def both(*conds):
    out = conds[0]
    for cond in conds[1:]:
        out = jnp.logical_and(out, cond)
    return out


def layer_kernel(tok, lng, win, mb, qs, ks, wout, ab, ob, out, buf, wi, wo, xv, zv, acc, att, qkv, act, mxb, stat,
                 lng_v, mb_v, qs_v, ks_v, ab_v, ob_v, bias_v,
                 wsem, xsem, psem, ssem, rsem, tsend, trecv, msend, mrecv, osem):
    dp = lax.axis_index("dp")
    z = lax.axis_index("my")
    mx = lax.axis_index("mx")
    low = z < 2
    k = jnp.where(low, z, 3 - z)
    side = jnp.where(low, 0, 1)
    inner = jnp.where(low, z + 1, z - 1)
    outer = jnp.where(k == 0, inner, jnp.where(low, z - 1, z + 1))
    core_peer = mx + 1 - 2 * (mx % 2)
    y_peer = (mx + 2) % 4
    near = SIDE_W * side
    far = SIDE_W * (1 - side)

    def win_copy(col, width, idx):
        cols = pl.ds(pl.multiple_of(col, 128), width)
        return pltpu.make_async_copy(win.at[:, cols], wi.at[:, cols], wsem.at[idx])

    def qkv_copy(t, base, idx):
        return win_copy(t * QKV_W + base, SIDE_W, idx)

    def up_copy(j):
        return win_copy(3 * QKV_W + j * CW, CW, 6 + j)

    def attn_w_copy():
        return pltpu.make_async_copy(wout.at[pl.ds(0, QKV_W)], wo.at[pl.ds(0, QKV_W)], wsem.at[6 + NJ])

    def down_copy(j):
        rows = pl.ds(pl.multiple_of(QKV_W + j * CW, 128), CW)
        return pltpu.make_async_copy(wout.at[rows], wo.at[rows], wsem.at[7 + NJ + j])

    x_copy = pltpu.make_async_copy(tok.at[0], xv, xsem)
    x_copy.start()
    small = [pltpu.make_async_copy(a, b, psem.at[i]) for i, (a, b) in enumerate(
        ((lng, lng_v), (mb, mb_v), (qs, qs_v), (ks, ks_v), (ab, ab_v), (ob, ob_v)))]
    for copy in small:
        copy.start()

    barrier = pltpu.get_barrier_semaphore()
    for i in (3, 2, 1):
        pl.semaphore_signal(barrier, inc=1, device_id=(dp, (z + i) % 4, mx), device_id_type=MESH)
    for peer in (core_peer, y_peer):
        pl.semaphore_signal(barrier, inc=1, device_id=(dp, z, peer), device_id_type=MESH)

    for t in range(3):
        qkv_copy(t, far, t).start()

    x_copy.wait()
    xf = xv[...].astype(F32)
    mu = jnp.sum(xf, axis=1, keepdims=True) * (1.0 / DL)
    m2 = jnp.sum(jnp.square(xf - mu), axis=1, keepdims=True)
    lane = lax.broadcasted_iota(jnp.int32, (SEQ, 128), 1)
    stat[z] = jnp.where(lane == 0, mu, m2).T[:8]
    pl.semaphore_wait(barrier, 5)

    def stat_copy(i):
        return pltpu.make_async_remote_copy(
            src_ref=stat.at[z], dst_ref=stat.at[z], send_sem=tsend.at[i], recv_sem=trecv.at[z],
            device_id=(dp, (z + i) % 4, mx), device_id_type=MESH)

    for i in (3, 2, 1):
        stat_copy(i).start()
    acc[...] = jnp.zeros_like(acc)
    for copy in small:
        copy.wait()
    bias_v[...] = mb_v[...].astype(F32).reshape(NJ, CW)
    ln_gain = lng_v[...].astype(F32).reshape(1, DL)
    for t in range(3):
        qkv_copy(t, far, t).wait()
    for i in range(1, 4):
        src = (z + i) % 4
        pltpu.make_async_copy(stat.at[src], stat.at[src], trecv.at[src]).wait()
    for t in range(3):
        qkv_copy(t, near, 3 + t).start()
    means = [stat[i][0:1] for i in range(4)]
    devs = [stat[i][1:2] for i in range(4)]
    mean = (means[0] + means[1] + means[2] + means[3]) * 0.25
    m2_all = devs[0] + devs[1] + devs[2] + devs[3]
    for i in range(4):
        m2_all = m2_all + DL * jnp.square(means[i] - mean)
    inv = lax.rsqrt(m2_all * (1.0 / DTOT) + 1e-6)
    row = lax.broadcasted_iota(jnp.int32, (128, SEQ), 0)
    cols2 = jnp.where(row == 0, mean, inv).T
    zv[...] = ((xv[...].astype(F32) - cols2[:, 0:1]) * cols2[:, 1:2] * ln_gain).astype(BF16)

    def qkv_block(b, base, first):
        t, c, width = BLOCKS[b]
        cols = pl.ds(pl.multiple_of(t * QKV_W + base + c, 128), width)
        part = jnp.dot(zv[...], wi[:, cols], preferred_element_type=F32).astype(BF16)
        for h in range(width // HD):
            for i in range(4):
                buf[first + HALF_H * t + c // HD + h, :, HD * i:HD * (i + 1)] = part[
                    UR * i:UR * (i + 1), HD * h:HD * (h + 1)]

    def mlp_chunk(j):
        up_copy(j).wait()
        cols = pl.ds(pl.multiple_of(3 * QKV_W + j * CW, 128), CW)
        part = jnp.dot(zv[...], wi[:, cols], preferred_element_type=F32).astype(BF16)
        buf[MLP + 2 * j] = part[0:64]
        buf[MLP + 2 * j + 1] = part[64:128]
        buf[MLP + 20 + j] = part[128:192]
        rows = pl.ds(pl.multiple_of(32 * (j % 2), 32), 32)
        buf[MLP + 30 + j // 2, rows] = part[192:224]
        buf[MLP + 35 + j // 2, rows] = part[224:256]

    def unit_copy(src, dst, which, dst_which, u, target):
        return pltpu.make_async_remote_copy(
            src_ref=buf.at[src], dst_ref=buf.at[dst], send_sem=ssem.at[which, u], recv_sem=rsem.at[dst_which, u],
            device_id=(dp, target, mx), device_id_type=MESH)

    def arrival(slot, which, u):
        return pltpu.make_async_copy(buf.at[slot], buf.at[slot], rsem.at[which, u])

    def kind(u):
        is_q = u < NQ
        is_a = both(u >= A0, u < A0 + NA)
        m = u - NQ - jnp.where(u >= A0 + NA, NA, 0)
        return is_q, is_a, m

    def put_attention(which, u, unit):
        cols = pl.ds(pl.multiple_of((u - A0) * HD, HD), HD)
        for i in range(4):
            att[which, UR * i:UR * (i + 1), cols] = unit[:, HD * i:HD * (i + 1)]

    def activate(h, j):
        pre = h.astype(BF16).astype(F32) + bias_v[pl.ds(j, 1), :]
        return (0.5 * pre * (1.0 + lax.erf(pre * (0.5 ** 0.5)))).astype(BF16)

    def down(g, first_row, j):
        r0, rows, _ = GROUPS[g]
        w0 = pl.multiple_of(QKV_W + j * CW, 128)
        for n in range(DL // 256):
            acc[r0:r0 + rows, 256 * n:256 * (n + 1)] += jnp.dot(
                act[first_row:first_row + rows, :], wo[pl.ds(w0, CW), 256 * n:256 * (n + 1)],
                preferred_element_type=F32)

    def mx_copy(step, g):
        rows = pl.ds(GROUPS[g][0], GROUPS[g][1])
        return pltpu.make_async_remote_copy(
            src_ref=mxb.at[2 * step, rows], dst_ref=mxb.at[2 * step + 1, rows],
            send_sem=msend.at[step, g], recv_sem=mrecv.at[step, g],
            device_id=(dp, z, (core_peer, y_peer)[step]), device_id_type=MESH)

    def out_copy(g):
        rows = pl.ds(GROUPS[g][0], GROUPS[g][1])
        return pltpu.make_async_copy(xv.at[rows], out.at[0, rows], osem.at[g])

    def reduce_a(g):
        r0, rows, _ = GROUPS[g]
        mxb[0, r0:r0 + rows] = acc[r0:r0 + rows].astype(BF16)
        mx_copy(0, g).start()

    def reduce_b(g):
        r0, rows, _ = GROUPS[g]
        mx_copy(0, g).wait()
        mxb[2, r0:r0 + rows] = (mxb[0, r0:r0 + rows].astype(F32) + mxb[1, r0:r0 + rows].astype(F32)).astype(BF16)
        mx_copy(1, g).start()

    def reduce_c(g):
        r0, rows, _ = GROUPS[g]
        bias = (ab_v[...].astype(F32) + ob_v[...].astype(F32)).reshape(1, DL)
        mx_copy(1, g).wait()
        total = mxb[2, r0:r0 + rows].astype(F32) + mxb[3, r0:r0 + rows].astype(F32)
        xv[r0:r0 + rows] = (total + bias + xv[r0:r0 + rows].astype(F32)).astype(BF16)
        out_copy(g).start()

    qkv_block(0, far, FAR)

    late_lag = (3 - k) * HOP
    near_first = 3
    mlp_first = near_first + len(BLOCKS) - 2

    def step(s, carry):
        for b in range(1, len(BLOCKS)):
            @pl.when(s == b - 1)
            def _():
                qkv_block(b, far, FAR)

        @pl.when(both(s >= 1, s < 1 + NJ))
        def _():
            up_copy(s - 1).start()

        @pl.when(s == 12)
        def _():
            attn_w_copy().start()

        @pl.when(both(s >= 14, s < 14 + NJ))
        def _():
            down_copy(s - 14).start()

        ue = s - k * HOP

        @pl.when(both(ue >= 0, ue < NU))
        def _():
            is_q, is_a, m = kind(ue)
            own = jnp.where(is_q, FAR + ue, MLP + m)
            slot = EARLY + ue

            @pl.when(k == 1)
            def _():
                arrival(slot, 0, ue).wait()

                @pl.when(jnp.logical_not(is_a))
                def _():
                    buf[slot] = (buf[slot].astype(F32) + buf[own].astype(F32)).astype(BF16)

            src = jnp.where(jnp.logical_or(k == 1, is_a), slot, own)
            unit_copy(src, jnp.where(k == 0, EARLY, LATE) + ue, 0, k, ue, inner).start()

            @pl.when(both(k == 1, is_a))
            def _():
                put_attention(0, ue, buf[slot])

        for b in range(len(BLOCKS)):
            @pl.when(s == near_first + b)
            def _():
                if b % 3 == 0:
                    qkv_copy(b // 3, near, 3 + b // 3).wait()
                qkv_block(b, near, NEAR)

        @pl.when(both(s >= mlp_first, s < mlp_first + 2 * NJ, (s - mlp_first) % 2 == 0))
        def _():
            mlp_chunk((s - mlp_first) // 2)

        ul = s - late_lag

        @pl.when(both(ul >= 0, ul < NU))
        def _():
            is_q, is_a, m = kind(ul)
            own = jnp.where(is_q, NEAR + ul, MLP + m)
            slot = LATE + ul
            arrival(slot, 1, ul).wait()
            is_m = jnp.logical_not(jnp.logical_or(is_q, is_a))
            g = jnp.where(m < 20, 0, jnp.where(m < 30, 1, jnp.where(m < 35, 2, 3)))
            pair = 2 * (m - jnp.where(g == 2, 30, 35))
            top = jnp.where(g == 0, m // 2, jnp.where(g == 1, m - 20, pair))
            bottom = jnp.where(g < 2, top, pair + 1)
            arow = pl.multiple_of(jnp.where(g == 0, UR * (m % 2), 0), UR)

            @pl.when(is_m)
            def _():
                other = jnp.where(k == 0, own, EARLY + ul)
                h = buf[slot].astype(F32) + buf[other].astype(F32)
                act[pl.ds(arow, UR), :] = jnp.concatenate(
                    [activate(h[0:32], top), activate(h[32:64], bottom)], axis=0)

            @pl.when(k == 1)
            def _():
                @pl.when(jnp.logical_not(is_a))
                def _():
                    buf[slot] = (buf[slot].astype(F32) + buf[own].astype(F32)).astype(BF16)

                unit_copy(slot, slot, 1, 1, ul, outer).start()

            @pl.when(is_a)
            def _():
                put_attention(1, ul, buf[slot])

            @pl.when(both(k == 0, is_q))
            def _():
                whole = (buf[slot].astype(F32) + buf[own].astype(F32)).astype(BF16)
                for q in range(4):
                    qkv[ul, UR * q:UR * (q + 1), :] = whole[:, HD * q:HD * (q + 1)]

            @pl.when(both(is_m, g == 0, m % 2 == 1))
            def _():
                down_copy(top).wait()
                down(0, 0, top)

            @pl.when(both(is_m, g == 1))
            def _():
                down(1, 0, top)

            for gg in (2, 3):
                @pl.when(both(is_m, g == gg))
                def _():
                    down(gg, 0, top)
                    down(gg, 32, bottom)

            for gg in range(NG):
                @pl.when(ul == GROUP_END[gg])
                def _():
                    reduce_a(gg)

            for gg in range(NG - 1):
                @pl.when(ul == GROUP_END[gg] + 2)
                def _():
                    reduce_b(gg)

            @pl.when(ul == GROUP_END[0] + 9)
            def _():
                reduce_c(0)

            @pl.when(ul == GROUP_END[1] + 7)
            def _():
                reduce_c(1)

        head = ul - 2 * HALF_H

        @pl.when(both(k == 0, head >= 0, head < HALF_H))
        def _():
            query = head_norm(qkv[head], qs_v[...].astype(F32).reshape(1, HD))
            key = head_norm(qkv[HALF_H + head], ks_v[...].astype(F32).reshape(1, HD))
            logits = lax.dot_general(query, key, (((1,), (1,)), ((), ())), preferred_element_type=F32) * (HD ** -0.5)
            expo = jnp.exp(logits - jnp.max(logits, axis=-1, keepdims=True))
            prob = (expo / jnp.sum(expo, axis=-1, keepdims=True)).astype(BF16)
            mixed = jnp.dot(prob, qkv[2 * HALF_H + head], preferred_element_type=F32).astype(BF16)
            att[0, :, pl.ds(pl.multiple_of(head * HD, HD), HD)] = mixed
            for q in range(4):
                buf[EARLY + A0 + head, :, HD * q:HD * (q + 1)] = mixed[UR * q:UR * (q + 1)]

        n = ul - (A0 + NA)

        @pl.when(n == 0)
        def _():
            attn_w_copy().wait()

        @pl.when(both(n >= 0, n < DL // 256))
        def _():
            cols = pl.ds(pl.multiple_of(n * 256, 256), 256)
            near_rows = pl.ds(pl.multiple_of(near, HD), SIDE_W)
            far_rows = pl.ds(pl.multiple_of(far, HD), SIDE_W)
            acc[:, cols] += (jnp.dot(att[0], wo[near_rows, cols], preferred_element_type=F32)
                             + jnp.dot(att[1], wo[far_rows, cols], preferred_element_type=F32))

        return carry

    lax.fori_loop(0, NU + late_lag, step, 0)
    reduce_b(3)
    reduce_c(2)

    def drain(u, carry):
        unit_copy(0, 0, 0, 0, u, inner).wait_send()

        @pl.when(k == 1)
        def _():
            unit_copy(0, 0, 1, 1, u, outer).wait_send()

        return carry

    lax.fori_loop(0, NU, drain, 0)
    for i in range(1, 4):
        stat_copy(i).wait_send()
    reduce_c(3)
    for g in range(NG):
        out_copy(g).wait()


def solution(mesh):
    def local_layer(tokens, ln_scale, w_in, mlp_bias, q_scale, k_scale, w_out, attn_out_bias, mlp_out_bias):
        dma = pltpu.SemaphoreType.DMA
        vmem = pltpu.VMEM
        return pl.pallas_call(
            layer_kernel,
            out_shape=jax.ShapeDtypeStruct((1, SEQ, DL), BF16),
            in_specs=[pl.BlockSpec(memory_space=pl.ANY)] * 9,
            out_specs=pl.BlockSpec(memory_space=pl.ANY),
            scratch_shapes=[
                vmem((NBUF, UR, CW), BF16),
                vmem((DL, 3 * QKV_W + FFB), BF16),
                vmem((QKV_W + FFB, DL), BF16),
                vmem((SEQ, DL), BF16),
                vmem((SEQ, DL), BF16),
                vmem((SEQ, DL), F32),
                vmem((2, SEQ, SIDE_W), BF16),
                vmem((3 * HALF_H, SEQ, HD), BF16),
                vmem((128, CW), BF16),
                vmem((4, SEQ, DL), BF16),
                vmem((4, 8, SEQ), F32),
                vmem((DL,), BF16),
                vmem((FFB,), BF16),
                vmem((HD,), BF16),
                vmem((HD,), BF16),
                vmem((DL,), BF16),
                vmem((DL,), BF16),
                vmem((NJ, CW), F32),
                dma((7 + 2 * NJ,)),
                dma,
                dma((6,)),
                dma((2, NU)),
                dma((2, NU)),
                dma((4,)),
                dma((4,)),
                dma((2, NG)),
                dma((2, NG)),
                dma((NG,)),
            ],
            compiler_params=pltpu.CompilerParams(
                collective_id=0, has_side_effects=True, vmem_limit_bytes=67043328),
            name="layer",
        )(tokens, ln_scale, w_in, mlp_bias, q_scale, k_scale, w_out, attn_out_bias, mlp_out_bias)

    specs_in = (P('dp', None, 'my'), P('my'), P('my', 'mx'), P('mx'), P(), P(), P('mx', 'my'), P('my'), P('my'))
    return jax.shard_map(local_layer, mesh=mesh, in_specs=specs_in, out_specs=P('dp', None, 'my'), check_vma=False)
```

time: 133 us -> 115 us (0.86); the launches traced: 131 us -> 114 us
  Pallas kernels: 124 us -> 112 us
  other arithmetic: 3.43 us -> 0 us
    pallas_call x1, Pallas kernels: 124 us -> 112 us  [local_layer(): pl.pallas_call(layer_kernel, out_shape=jax.ShapeDtypeStruct((1, SEQ, DL),...]
    unnamed x5 -> x0, other arithmetic: 3.43 us -> none
where the time goes in v2:
time: 115 us; the launch traced here: 114 us
  Pallas kernels  112 us (97%)
  local copies, waits for them, and re-layouts  1.97 us (2%)
    pallas_call x1, Pallas kernels, local_layer(): pl.pallas_call(layer_kernel, out_shape=jax.ShapeDtypeStruct((1, SEQ, DL),...  112 us

profile of v2, /device:TPU:1, one launch (start us, length us, event | category | flops | bytes accessed | tf_op | source)
XLA Modules:
  0.0 114.0 jit_solution(13373398039352829010)
XLA Ops:
  0.0 112.0 %layer.1 = bf16[1,256,1280]{2,1,0:T(8,128)(2,1)} custom-call(bf16[1,256,1280]{2,1,0:T(8,128)(2,1)} %tok.1, bf16[1280]{0:T(1024)(128)(2,1)} %lng.1, bf16[1280,8960]{1,0:T(8,128)(2,1)} %win.1, bf16[5120]{0:T(1024)(128)(2,1)} %mb.1, bf16[128]{0:T(256)(128)(2,1)} %qs.1, bf16[128]{0:T(256)(128)(2,1)} %ks.1, bf16[6400,1280]{1,0:T(8,128)(2,1)} %wout.1, ...), custom_call_target="tpu_custom_call" | custom-call | tf_op jit(solution)/shard_map/layer/pallas_call | solution.py:409
  112.1 2.0 %copy.11 = bf16[1,256,1280]{2,1,0:T(8,128)(2,1)} copy(bf16[1,256,1280]{2,1,0:T(8,128)(2,1)} %layer.1) | data formatting | bytes 1310720
